TPU v7x, 32 devices: a whole 2x2x4 slice. The times are simulated.
32 devices in a mesh: dp: 8 (over y, x, core), tensor: 4 (over z).
Axes of the slice: x: 2, y: 2, z: 4, core: 2. Of those that a mesh axis runs over, the one named last changes fastest.
Arguments:
- tokens: bfloat16 [4096, 1024], P(('dp', 'tensor')), may hold values from -5 to 5
- lengths: int32 [8, 2], P('dp'), may hold values from 0 to 512, as said below
- w_query: bfloat16 [1024, 1024], P('dp', 'tensor'), may hold values from -0.1875 to 0.1875
- b_query: float32 [1024], replicated, may hold values from -3 to 3
- w_key: bfloat16 [1024, 1024], P('dp', 'tensor'), may hold values from -0.1875 to 0.1875
- w_value: bfloat16 [1024, 1024], P('dp', 'tensor'), may hold values from -0.1875 to 0.1875
- b_value: float32 [1024], replicated, may hold values from -3 to 3
- w_out: bfloat16 [1024, 1024], P('tensor', 'dp'), may hold values from -3 to 3
- b_out: float32 [1024], replicated, may hold values from -3 to 3
- gain_attn: float32 [1024], replicated, may hold values from 0.1 to 1.9
- shift_attn: float32 [1024], replicated, may hold values from -3 to 3
- w_in: bfloat16 [1024, 4096], P('dp', 'tensor'), may hold values from -0.1875 to 0.1875
- b_in: float32 [4096], replicated, may hold values from -3 to 3
- w_back: bfloat16 [4096, 1024], P('tensor', 'dp'), may hold values from -0.09375 to 0.09375
- b_back: float32 [1024], replicated, may hold values from -3 to 3
- gain_ffn: float32 [1024], replicated, may hold values from 0.1 to 1.9
- shift_ffn: float32 [1024], replicated, may hold values from -3 to 3
- cotangent: bfloat16 [4096, 1024], P(('dp', 'tensor')), may hold values from -6 to 6
Outputs:
- output: bfloat16 [4096, 1024], P(('dp', 'tensor'))
- grad_tokens: float32 [4096, 1024], P(('dp', 'tensor'))
- grad_w_query: float32 [1024, 1024], P('dp', 'tensor')
- grad_b_query: float32 [1024], replicated
- grad_w_key: float32 [1024, 1024], P('dp', 'tensor')
- grad_w_value: float32 [1024, 1024], P('dp', 'tensor')
- grad_b_value: float32 [1024], replicated
- grad_w_out: float32 [1024, 1024], P('tensor', 'dp')
- grad_b_out: float32 [1024], replicated
- grad_gain_attn: float32 [1024], replicated
- grad_shift_attn: float32 [1024], replicated
- grad_w_in: float32 [1024, 4096], P('dp', 'tensor')
- grad_b_in: float32 [4096], replicated
- grad_w_back: float32 [4096, 1024], P('tensor', 'dp')
- grad_b_back: float32 [1024], replicated
- grad_gain_ffn: float32 [1024], replicated
- grad_shift_ffn: float32 [1024], replicated
Inputs may be any that keep to these rules, and one draw needn't show every extreme that they name: Each group's 2 lengths sum to at most 512; the first is 1 or more, the second may be 0; in every draw one group holds a single sequence of exactly 512 tokens.
All inputs are finite; a program needn't handle non-finite values.
Results may differ from a plain program's by a relative error of at most 0.02.
Values may be sent and summed in bfloat16 or wider, within the bound.
A program may use at most 128 MiB of HBM per device.

v0:
```python
import jax
import jax.numpy as jnp
from jax import lax
from jax.sharding import PartitionSpec as P

HD = 64
epsilon = 1e-06
masked_value = -1e30


def matmul_plain(left_side, right_side):
    return jnp.dot(left_side, right_side, preferred_element_type=jnp.float32)


def matmul_over_rows(left_side, right_side):
    return lax.dot_general(
        left_side, right_side, (((0,), (0,)), ((), ())), preferred_element_type=jnp.float32
    )


def matmul_over_cols(left_side, right_side):
    return lax.dot_general(
        left_side, right_side, (((1,), (1,)), ((), ())), preferred_element_type=jnp.float32
    )


def layer_norm(residual, gain_vec, shift_vec):
    mean_val = jnp.mean(residual, axis=-1, keepdims=True)
    centered = residual - mean_val
    inv_std = lax.rsqrt(jnp.mean(centered * centered, axis=-1, keepdims=True) + epsilon)
    normed = centered * inv_std
    return (normed * gain_vec + shift_vec, normed, inv_std)


def norm_back(grad_out, normed, inv_std, gain_vec):
    grad_norm = grad_out * gain_vec
    first_mean = jnp.mean(grad_norm, axis=-1, keepdims=True)
    second_mean = jnp.mean(grad_norm * normed, axis=-1, keepdims=True)
    return inv_std * (grad_norm - first_mean - normed * second_mean)


def gelu_parts(preact):
    cdf_val = 0.5 * (1.0 + lax.erf(preact * 0.7071067811865476))
    pdf_val = jnp.exp(-0.5 * preact * preact) * 0.3989422804014327
    return (preact * cdf_val, cdf_val + preact * pdf_val)


def attend_forward(query_rows, key_rows, value_rows, seg_ids, head_dim, block_rows):
    group_rows, head_cols = query_rows.shape
    pair_width = 2 * head_dim
    block_count = group_rows // block_rows
    pair_count = head_cols // pair_width
    score_scale = head_dim ** (-0.5)

    def attend_step(step_index, loop_carry):
        context, log_total = loop_carry
        pair_index = step_index // block_count
        row_start = step_index % block_count * block_rows
        first_col = pair_index * pair_width
        query_block = lax.dynamic_slice(
            query_rows, (row_start, first_col), (block_rows, pair_width)
        ).reshape(block_rows, 2, head_dim)
        key_pair = lax.dynamic_slice(key_rows, (0, first_col), (group_rows, pair_width)).reshape(
            group_rows, 2, head_dim
        )
        value_pair = lax.dynamic_slice(
            value_rows, (0, first_col), (group_rows, pair_width)
        ).reshape(group_rows, 2, head_dim)
        same_seg = seg_ids[:, None] == seg_ids[None, :]
        scores = (
            jnp.einsum("qhd,khd->hqk", query_block, key_pair, preferred_element_type=jnp.float32)
            * score_scale
        )
        scores = jnp.where(same_seg[None], scores, masked_value)
        row_max = jnp.max(scores, axis=-1, keepdims=True)
        block_total = row_max + jnp.log(jnp.sum(jnp.exp(scores - row_max), axis=-1, keepdims=True))
        prob_bf = jnp.exp(scores - block_total).astype(jnp.bfloat16)
        context_block = jnp.einsum(
            "hqk,khd->qhd", prob_bf, value_pair, preferred_element_type=jnp.float32
        ).astype(jnp.bfloat16)
        context = lax.dynamic_update_slice(
            context, context_block.reshape(block_rows, pair_width), (row_start, first_col)
        )
        log_total = lax.dynamic_update_slice(
            log_total, block_total[:, :, 0], (2 * pair_index, row_start)
        )
        return (context, log_total)

    start_carry = (
        jnp.zeros((group_rows, head_cols), jnp.bfloat16),
        jnp.zeros((head_cols // head_dim, group_rows), jnp.float32),
    )
    return lax.fori_loop(0, pair_count * block_count, attend_step, start_carry)


def attend_backward(
    query_rows,
    key_rows,
    value_rows,
    context,
    grad_context,
    log_total,
    seg_ids,
    head_dim,
    block_rows,
):
    group_rows, head_cols = query_rows.shape
    pair_width = 2 * head_dim
    block_count = group_rows // block_rows
    pair_count = head_cols // pair_width
    score_scale = head_dim ** (-0.5)

    def back_step(step_index, loop_carry):
        grad_query, grad_keys, grad_values = loop_carry
        pair_index = step_index // block_count
        row_start = step_index % block_count * block_rows
        first_col = pair_index * pair_width
        query_block = lax.dynamic_slice(
            query_rows, (row_start, first_col), (block_rows, pair_width)
        ).reshape(block_rows, 2, head_dim)
        key_pair = lax.dynamic_slice(key_rows, (0, first_col), (group_rows, pair_width)).reshape(
            group_rows, 2, head_dim
        )
        value_pair = lax.dynamic_slice(
            value_rows, (0, first_col), (group_rows, pair_width)
        ).reshape(group_rows, 2, head_dim)
        context_block = lax.dynamic_slice(
            context, (row_start, first_col), (block_rows, pair_width)
        ).reshape(block_rows, 2, head_dim)
        gctx_block = lax.dynamic_slice(
            grad_context, (row_start, first_col), (block_rows, pair_width)
        ).reshape(block_rows, 2, head_dim)
        total_block = lax.dynamic_slice(log_total, (2 * pair_index, row_start), (2, block_rows))
        same_seg = seg_ids[:, None] == seg_ids[None, :]
        scores = (
            jnp.einsum("qhd,khd->hqk", query_block, key_pair, preferred_element_type=jnp.float32)
            * score_scale
        )
        scores = jnp.where(same_seg[None], scores, masked_value)
        probs = jnp.exp(scores - total_block[:, :, None])
        prob_bf = probs.astype(jnp.bfloat16)
        grad_probs = jnp.einsum(
            "qhd,khd->hqk", gctx_block, value_pair, preferred_element_type=jnp.float32
        )
        delta_rows = jnp.sum(
            gctx_block.astype(jnp.float32) * context_block.astype(jnp.float32), axis=-1
        ).T[:, :, None]
        grad_scores = (probs * (grad_probs - delta_rows) * score_scale).astype(jnp.bfloat16)
        grad_q_block = jnp.einsum(
            "hqk,khd->qhd", grad_scores, key_pair, preferred_element_type=jnp.float32
        ).reshape(block_rows, pair_width)
        grad_k_pair = jnp.einsum(
            "hqk,qhd->khd", grad_scores, query_block, preferred_element_type=jnp.float32
        ).reshape(group_rows, pair_width)
        grad_v_pair = jnp.einsum(
            "hqk,qhd->khd", prob_bf, gctx_block, preferred_element_type=jnp.float32
        ).reshape(group_rows, pair_width)
        grad_query = lax.dynamic_update_slice(grad_query, grad_q_block, (row_start, first_col))
        old_keys = lax.dynamic_slice(grad_keys, (0, first_col), (group_rows, pair_width))
        grad_keys = lax.dynamic_update_slice(grad_keys, old_keys + grad_k_pair, (0, first_col))
        old_values = lax.dynamic_slice(grad_values, (0, first_col), (group_rows, pair_width))
        grad_values = lax.dynamic_update_slice(
            grad_values, old_values + grad_v_pair, (0, first_col)
        )
        return (grad_query, grad_keys, grad_values)

    zero_grad = jnp.zeros((group_rows, head_cols), jnp.float32)
    return lax.fori_loop(0, pair_count * block_count, back_step, (zero_grad, zero_grad, zero_grad))


def on_device(
    tokens,
    lengths,
    w_query,
    b_query,
    w_key,
    w_value,
    b_value,
    w_out,
    b_out,
    gain_attn,
    shift_attn,
    w_in,
    b_in,
    w_back,
    b_back,
    gain_ffn,
    shift_ffn,
    cotangent,
):
    tensor_size = lax.axis_size("tensor")
    tensor_index = lax.axis_index("tensor")
    local_rows = tokens.shape[0]
    group_rows = local_rows * tensor_size
    head_cols = w_query.shape[1]
    hidden_cols = w_in.shape[1]
    block_rows = min(512, group_rows)
    seq_lens = lengths[0]
    live_end = seq_lens[0] + seq_lens[1]
    positions = jnp.arange(group_rows, dtype=jnp.int32)
    seg_ids = (positions >= seq_lens[0]).astype(jnp.int32) + (positions >= live_end).astype(
        jnp.int32
    )
    local_pos = tensor_index * local_rows + jnp.arange(local_rows, dtype=jnp.int32)
    live_rows = (local_pos < live_end).astype(jnp.float32)[:, None]
    rows_full = lax.all_gather(tokens, "tensor", axis=0, tiled=True)
    attn_mats = (
        lax.all_gather(w_query, "dp", axis=0, tiled=True),
        lax.all_gather(w_key, "dp", axis=0, tiled=True),
        lax.all_gather(w_value, "dp", axis=0, tiled=True),
        lax.all_gather(w_out, "dp", axis=1, tiled=True),
    )
    mat_query, mat_key, mat_value, mat_out = attn_mats
    bias_query = lax.dynamic_slice_in_dim(b_query, tensor_index * head_cols, head_cols)
    bias_value = lax.dynamic_slice_in_dim(b_value, tensor_index * head_cols, head_cols)
    bias_in = lax.dynamic_slice_in_dim(b_in, tensor_index * hidden_cols, hidden_cols)
    query_rows = (matmul_plain(rows_full, mat_query) + bias_query).astype(jnp.bfloat16)
    key_rows = matmul_plain(rows_full, mat_key).astype(jnp.bfloat16)
    value_rows = (matmul_plain(rows_full, mat_value) + bias_value).astype(jnp.bfloat16)
    context, log_total = attend_forward(query_rows, key_rows, value_rows, seg_ids, HD, block_rows)
    attn_sum = lax.psum_scatter(
        matmul_plain(context, mat_out).astype(jnp.bfloat16),
        "tensor",
        scatter_dimension=0,
        tiled=True,
    ).astype(jnp.float32)
    resid_one = tokens.astype(jnp.float32) + attn_sum + b_out
    hidden_one, normed_one, inv_one = layer_norm(resid_one, gain_attn, shift_attn)
    hidden_bf = hidden_one.astype(jnp.bfloat16)
    hidden_full = lax.all_gather(hidden_bf, "tensor", axis=0, tiled=True)
    ffn_mats = (
        lax.all_gather(w_in, "dp", axis=0, tiled=True),
        lax.all_gather(w_back, "dp", axis=1, tiled=True),
    )
    mat_in, mat_back = ffn_mats
    preact = matmul_plain(hidden_full, mat_in) + bias_in
    activ_val, gelu_slope = gelu_parts(preact)
    activation = activ_val.astype(jnp.bfloat16)
    ffn_sum = lax.psum_scatter(
        matmul_plain(activation, mat_back).astype(jnp.bfloat16),
        "tensor",
        scatter_dimension=0,
        tiled=True,
    ).astype(jnp.float32)
    resid_two = hidden_one + ffn_sum + b_back
    normed_out, normed_two, inv_two = layer_norm(resid_two, gain_ffn, shift_ffn)
    output = (normed_out * live_rows).astype(jnp.bfloat16)
    grad_final = cotangent.astype(jnp.float32) * live_rows
    grad_gain_ffn = jnp.sum(grad_final * normed_two, axis=0)
    grad_shift_ffn = jnp.sum(grad_final, axis=0)
    grad_two = norm_back(grad_final, normed_two, inv_two, gain_ffn)
    grad_b_back = jnp.sum(grad_two, axis=0)
    mat_query, mat_key, mat_value, mat_out, mat_in, mat_back = (
        lax.all_gather(w_query, "dp", axis=0, tiled=True),
        lax.all_gather(w_key, "dp", axis=0, tiled=True),
        lax.all_gather(w_value, "dp", axis=0, tiled=True),
        lax.all_gather(w_out, "dp", axis=1, tiled=True),
        lax.all_gather(w_in, "dp", axis=0, tiled=True),
        lax.all_gather(w_back, "dp", axis=1, tiled=True),
    )
    grad_two_full = lax.all_gather(grad_two.astype(jnp.bfloat16), "tensor", axis=0, tiled=True)
    grad_w_back = matmul_over_rows(activation, grad_two_full)
    grad_pre = matmul_over_cols(grad_two_full, mat_back) * gelu_slope
    grad_b_in_part = jnp.sum(grad_pre, axis=0)
    grad_pre_bf = grad_pre.astype(jnp.bfloat16)
    grad_w_in = matmul_over_rows(hidden_full, grad_pre_bf)
    grad_one_out = grad_two + lax.psum_scatter(
        matmul_over_cols(grad_pre_bf, mat_in).astype(jnp.bfloat16),
        "tensor",
        scatter_dimension=0,
        tiled=True,
    ).astype(jnp.float32)
    grad_w_in, grad_w_back = (
        lax.psum_scatter(grad_w_in, "dp", scatter_dimension=0, tiled=True),
        lax.psum_scatter(grad_w_back, "dp", scatter_dimension=1, tiled=True),
    )
    grad_gain_attn = jnp.sum(grad_one_out * normed_one, axis=0)
    grad_shift_attn = jnp.sum(grad_one_out, axis=0)
    grad_one = norm_back(grad_one_out, normed_one, inv_one, gain_attn)
    grad_b_out = jnp.sum(grad_one, axis=0)
    grad_one_full = lax.all_gather(grad_one.astype(jnp.bfloat16), "tensor", axis=0, tiled=True)
    grad_w_out = matmul_over_rows(context, grad_one_full)
    grad_context = matmul_over_cols(grad_one_full, mat_out).astype(jnp.bfloat16)
    grad_query, grad_keys, grad_values = attend_backward(
        query_rows, key_rows, value_rows, context, grad_context, log_total, seg_ids, HD, block_rows
    )
    grad_b_query_part = jnp.sum(grad_query, axis=0)
    grad_b_value_part = jnp.sum(grad_values, axis=0)
    grad_query_bf = grad_query.astype(jnp.bfloat16)
    grad_keys_bf = grad_keys.astype(jnp.bfloat16)
    grad_values_bf = grad_values.astype(jnp.bfloat16)
    grad_w_query = matmul_over_rows(rows_full, grad_query_bf)
    grad_w_key = matmul_over_rows(rows_full, grad_keys_bf)
    grad_w_value = matmul_over_rows(rows_full, grad_values_bf)
    query_part = matmul_over_cols(grad_query_bf, mat_query)
    key_part = matmul_over_cols(grad_keys_bf, mat_key)
    value_part = matmul_over_cols(grad_values_bf, mat_value)
    grad_in = grad_one + lax.psum_scatter(
        (query_part + key_part + value_part).astype(jnp.bfloat16),
        "tensor",
        scatter_dimension=0,
        tiled=True,
    ).astype(jnp.float32)
    grad_w_query, grad_w_key, grad_w_value, grad_w_out = (
        lax.psum_scatter(grad_w_query, "dp", scatter_dimension=0, tiled=True),
        lax.psum_scatter(grad_w_key, "dp", scatter_dimension=0, tiled=True),
        lax.psum_scatter(grad_w_value, "dp", scatter_dimension=0, tiled=True),
        lax.psum_scatter(grad_w_out, "dp", scatter_dimension=1, tiled=True),
    )

    def widen(part_vec, full_width):
        return lax.dynamic_update_slice_in_dim(
            jnp.zeros((full_width,), jnp.float32), part_vec, tensor_index * part_vec.shape[0], 0
        )

    small_sums = lax.psum(
        (
            widen(grad_b_query_part, b_query.shape[0]),
            widen(grad_b_value_part, b_value.shape[0]),
            grad_b_out,
            grad_gain_attn,
            grad_shift_attn,
            widen(grad_b_in_part, b_in.shape[0]),
            grad_b_back,
            grad_gain_ffn,
            grad_shift_ffn,
        ),
        ("dp", "tensor"),
    )
    return (
        output,
        grad_in,
        grad_w_query,
        small_sums[0],
        grad_w_key,
        grad_w_value,
        small_sums[1],
        grad_w_out,
        small_sums[2],
        small_sums[3],
        small_sums[4],
        grad_w_in,
        small_sums[5],
        grad_w_back,
        small_sums[6],
        small_sums[7],
        small_sums[8],
    )


def solution(mesh):
    placed = (
        P(("dp", "tensor"), None),
        P("dp", None),
        P("dp", "tensor"),
        P(),
        P("dp", "tensor"),
        P("dp", "tensor"),
        P(),
        P("tensor", "dp"),
        P(),
        P(),
        P(),
        P("dp", "tensor"),
        P(),
        P("tensor", "dp"),
        P(),
        P(),
        P(),
        P(("dp", "tensor"), None),
    )
    return jax.shard_map(
        on_device,
        mesh=mesh,
        in_specs=placed,
        out_specs=(
            P(("dp", "tensor"), None),
            P(("dp", "tensor"), None),
            P("dp", "tensor"),
            P(),
            P("dp", "tensor"),
            P("dp", "tensor"),
            P(),
            P("tensor", "dp"),
            P(),
            P(),
            P(),
            P("dp", "tensor"),
            P(),
            P("tensor", "dp"),
            P(),
            P(),
            P(),
        ),
        check_vma=False,
    )
```

profile of v0, /device:TPU:0, one launch (start us, length us, event | category | flops | bytes accessed | tf_op | source)
XLA Modules:
  0.0 598.6 jit_solution(13437722508312491656)
XLA Ops:
  10.3 1.3 fusion.36
  13.0 11.6 %all_gather.37 = bf16[1024,256]{1,0:T(8,128)(2,1)S(1)} all-gather(bf16[128,256]{1,0:T(8,128)(2,1)} %param.27), channel_id=1, replica_groups=mesh['dp'=8,'tensor'=4] {'dp'}, dimensions={0}, use_global_device_ids=true | all-gather | bytes 589824 | tf_op jit(solution)/shard_map/all_gather | solution.py:210
  24.6 9.5 %all_gather.38 = bf16[1024,256]{1,0:T(8,128)(2,1)S(1)} all-gather(bf16[128,256]{1,0:T(8,128)(2,1)} %param.24), channel_id=1, replica_groups=mesh['dp'=8,'tensor'=4] {'dp'}, dimensions={0}, use_global_device_ids=true | all-gather | bytes 589824 | tf_op jit(solution)/shard_map/all_gather | solution.py:208
  34.1 9.2 %all_gather.39 = bf16[1024,256]{1,0:T(8,128)(2,1)S(1)} all-gather(bf16[128,256]{1,0:T(8,128)(2,1)} %param.26), channel_id=1, replica_groups=mesh['dp'=8,'tensor'=4] {'dp'}, dimensions={0}, use_global_device_ids=true | all-gather | bytes 589824 | tf_op jit(solution)/shard_map/all_gather | solution.py:209
  43.3 10.6 %all_gather.40 = bf16[256,1024]{1,0:T(8,128)(2,1)} all-gather(bf16[256,128]{1,0:T(8,128)(2,1)S(1)} %copy-done.33), channel_id=1, replica_groups=mesh['dp'=8,'tensor'=4] {'dp'}, dimensions={1}, use_global_device_ids=true | all-gather | bytes 589824 | tf_op jit(solution)/shard_map/all_gather | solution.py:211
  53.9 1.8 fusion.13
  57.1 4.8 while.38
  61.9 2.5 convolution_convert_fusion.3
  65.1 27.1 %reduce-scatter.11.cloned.1.call-done = bf16[128,1024]{1,0:T(8,128)(2,1)} async-done(((bf16[512,1024]{1,0:T(8,128)(2,1)}), bf16[128,1024]{1,0:T(8,128)(2,1)}) %reduce-scatter.11.cloned.1.call-update) | async-done | bytes 262160 | tf_op jit(solution)/shard_map/reduce_scatter | solution.py:221
  92.2 1.1 fusion.22
  93.3 1.2 multiply_reduce_fusion.5
  94.5 1.8 fusion.21
  97.6 27.1 %all-gather.9.cloned.1.call-done = bf16[512,1024]{1,0:T(8,128)(2,1)} async-done(((bf16[128,1024]{1,0:T(8,128)(2,1)}), bf16[512,1024]{1,0:T(8,128)(2,1)}) %all-gather.9.cloned.1.call-update) | async-done | bytes 1048592 | tf_op jit(solution)/shard_map/all_gather | solution.py:230
  124.7 4.6 multiply_convert_fusion.1
  129.3 24.4 %all-gather.13.cloned.1.call-done = bf16[1024,1024]{1,0:T(8,128)(2,1)} async-done(((bf16[1024,128]{1,0:T(8,128)(2,1)}), bf16[1024,1024]{1,0:T(8,128)(2,1)}) %all-gather.13.cloned.1.call-update) | async-done | bytes 2097168 | tf_op jit(solution)/shard_map/all_gather | solution.py:233
  153.8 3.9 convolution_convert_fusion.2
  157.7 27.4 %reduce-scatter.13.cloned.1.call-done = bf16[128,1024]{1,0:T(8,128)(2,1)} async-done(((bf16[512,1024]{1,0:T(8,128)(2,1)}), bf16[128,1024]{1,0:T(8,128)(2,1)}) %reduce-scatter.13.cloned.1.call-update) | async-done | bytes 262160 | tf_op jit(solution)/shard_map/reduce_scatter | solution.py:239
  185.1 1.3 fusion.34
  187.0 1.1 fusion.33
  188.3 26.4 %all-gather.15.cloned.1.call-done = bf16[512,1024]{1,0:T(8,128)(2,1)} async-done(((bf16[128,1024]{1,0:T(8,128)(2,1)}), bf16[512,1024]{1,0:T(8,128)(2,1)}) %all-gather.15.cloned.1.call-update) | async-done | bytes 1048592 | tf_op jit(solution)/shard_map/all_gather | solution.py:261
  214.7 5.2 fusion.37
  220.9 2.3 convolution_convert_fusion.1
  223.3 26.8 %reduce-scatter.15.cloned.1.call-done = bf16[128,1024]{1,0:T(8,128)(2,1)} async-done(((bf16[512,1024]{1,0:T(8,128)(2,1)}), bf16[128,1024]{1,0:T(8,128)(2,1)}) %reduce-scatter.15.cloned.1.call-update) | async-done | bytes 262160 | tf_op jit(solution)/shard_map/reduce_scatter | solution.py:267
  250.0 2.0 multiply_reduce_fusion.1
  252.0 1.8 fusion.32
  254.7 26.5 %all-gather.17.cloned.1.call-done = bf16[512,1024]{1,0:T(8,128)(2,1)} async-done(((bf16[128,1024]{1,0:T(8,128)(2,1)}), bf16[512,1024]{1,0:T(8,128)(2,1)}) %all-gather.17.cloned.1.call-update) | async-done | bytes 1048592 | tf_op jit(solution)/shard_map/all_gather | solution.py:281
  281.2 2.4 convolution_convert_fusion.4
  284.6 13.1 %while.39 = (s32[]{:T(128)}, f32[512,256]{0,1:T(8,128)}, f32[512,256]{0,1:T(8,128)S(1)}, f32[512,256]{0,1:T(8,128)S(1)}, bf16[512,256]{0,1:T(8,128)(2,1)S(1)}, /...) while((s32[]{:T(128)}, f32[512,256]{0,1:T(8,128)}, ...), condition=%wide.region_17.18_spmd.clone, body=%wide.region_15.17_spmd.clone.sunk | while | flops 340395520 | bytes 25846364 | solution.py:168
  297.7 2.9 convolution_bitcast_fusion.2
  300.7 1.4 convolution_bitcast_fusion.1
  302.2 1.5 convolution_bitcast_fusion
  304.8 1.6 fusion.29
  306.4 1.5 add_convert_fusion
  307.9 1.4 fusion.40
  309.5 4.5 fusion.41
  315.5 3.3 fusion.15
  319.6 1.2 reduce_sum.193
  321.4 41.4 %all-reduce = (f32[1024]{0:T(1024)}, f32[1024]{0:T(1024)}, f32[1024]{0:T(1024)}, f32[1024]{0:T(1024)}, f32[1024]{0:T(1024)}, /*index=5*/f32[4096]{0:T(1024)}, f32[1024]{0:T(1024)}, f32[1024]{0:T(1024)}, f32[1024]{0:T(1024)}) all-reduce(f32[1024]{0:T(1024)S(1)} %dynamic_update_slice.62, ...), channel_id=1, replica_groups=mesh['dp'=8,'tensor'=4] {'dp','tensor'}, use_global_device_ids=true, to_apply=%region_21.22 | all-reduce | flops 12288 | bytes 98304 | tf_op jit(solution)/shard_map/psum | solution.py:316
  362.8 1.7 copy.43
  364.4 10.7 %reduce-scatter.21.cloned.1.call-done = f32[128,256]{0,1:T(8,128)} async-done(((f32[1024,256]{0,1:T(8,128)}), f32[128,256]{0,1:T(8,128)}) %reduce-scatter.21.cloned.1.call-update) | async-done | bytes 131088 | tf_op jit(solution)/shard_map/reduce_scatter | solution.py:306
  375.2 1.7 copy.44
  376.8 37.3 %reduce-scatter.23.cloned.1.call-done = f32[128,256]{0,1:T(8,128)} async-done(((f32[1024,256]{0,1:T(8,128)}), f32[128,256]{0,1:T(8,128)}) %reduce-scatter.23.cloned.1.call-update) | async-done | bytes 131088 | tf_op jit(solution)/shard_map/reduce_scatter | solution.py:307
  414.1 1.7 copy.45
  415.8 27.8 %reduce-scatter.17.cloned.1.call-done = bf16[128,1024]{1,0:T(8,128)(2,1)} async-done(((bf16[512,1024]{1,0:T(8,128)(2,1)}), bf16[128,1024]{1,0:T(8,128)(2,1)}) %reduce-scatter.17.cloned.1.call-update) | async-done | bytes 262160 | tf_op jit(solution)/shard_map/reduce_scatter | solution.py:298
  443.6 1.8 convert_add_fusion.2
  445.4 36.2 %reduce-scatter.25.cloned.1.call-done = f32[256,128]{1,0:T(8,128)} async-done(((f32[256,1024]{1,0:T(8,128)}), f32[256,128]{1,0:T(8,128)}) %reduce-scatter.25.cloned.1.call-update) | async-done | bytes 131088 | tf_op jit(solution)/shard_map/reduce_scatter | solution.py:308
  481.6 54.9 %reduce-scatter.29.cloned.1.call-done = f32[1024,128]{1,0:T(8,128)} async-done(((f32[1024,1024]{1,0:T(8,128)}), f32[1024,128]{1,0:T(8,128)}) %reduce-scatter.29.cloned.1.call-update) | async-done | bytes 524304 | tf_op jit(solution)/shard_map/reduce_scatter | solution.py:275
  536.5 54.8 %reduce-scatter.27.cloned.1.call-done = f32[128,1024]{1,0:T(8,128)} async-done(((f32[1024,1024]{1,0:T(8,128)}), f32[128,1024]{1,0:T(8,128)}) %reduce-scatter.27.cloned.1.call-update) | async-done | bytes 524304 | tf_op jit(solution)/shard_map/reduce_scatter | solution.py:274
  (227 shorter events, 30.8 us)
Async XLA Ops:
  8.0 35.3 %copy-start.33 = (bf16[256,128]{1,0:T(8,128)(2,1)S(1)}, bf16[256,128]{1,0:T(8,128)(2,1)}, u32[]{:S(2)}) copy-start(bf16[256,128]{1,0:T(8,128)(2,1)} %param.29) | copy-start | bytes 196612
  8.0 45.8 %all-gather.7.cloned.1.call-start = ((), (), s32[]{:S(2)}) async-start(), calls=%async_computation.10 | async-start | bytes 1310720 | tf_op jit(solution)/shard_map/all_gather | solution.py:206
  8.8 83.4 %reduce-scatter.11.cloned.1.call-start = ((), (), s32[]{:S(2)}) async-start(), calls=%async_computation.11 | async-start | bytes 1310720 | tf_op jit(solution)/shard_map/reduce_scatter | solution.py:221
  24.6 31.2 %copy-start.16 = (bf16[1024,256]{1,0:T(8,128)(2,1)}, bf16[1024,256]{1,0:T(8,128)(2,1)S(1)}, u32[]{:S(2)}) copy-start(bf16[1024,256]{1,0:T(8,128)(2,1)S(1)} %all_gather.37) | copy-start | bytes 1572868
  34.1 22.2 %copy-start.19 = (bf16[1024,256]{1,0:T(8,128)(2,1)}, bf16[1024,256]{1,0:T(8,128)(2,1)S(1)}, u32[]{:S(2)}) copy-start(bf16[1024,256]{1,0:T(8,128)(2,1)S(1)} %all_gather.38) | copy-start | bytes 1572868
  43.3 13.1 %copy-start.21 = (bf16[1024,256]{1,0:T(8,128)(2,1)}, bf16[1024,256]{1,0:T(8,128)(2,1)S(1)}, u32[]{:S(2)}) copy-start(bf16[1024,256]{1,0:T(8,128)(2,1)S(1)} %all_gather.39) | copy-start | bytes 1572868
  53.9 1.9 copy-start.9
  61.8 30.3 %copy-start.2 = (bf16[128,1024]{1,0:T(8,128)(2,1)S(1)}, bf16[128,1024]{1,0:T(8,128)(2,1)}, u32[]{:S(2)}) copy-start(bf16[128,1024]{1,0:T(8,128)(2,1)} %param.22) | copy-start | bytes 786436
  61.9 30.3 %copy-start.31 = (f32[1024]{0:T(1024)S(1)}, f32[1024]{0:T(1024)}, u32[]{:S(2)}) copy-start(f32[1024]{0:T(1024)} %param.30) | copy-start | bytes 12292
  61.9 32.6 %copy-start.32 = (f32[1024]{0:T(1024)S(1)}, f32[1024]{0:T(1024)}, u32[]{:S(2)}) copy-start(f32[1024]{0:T(1024)} %param.31) | copy-start | bytes 12292
  61.9 32.6 %copy-start.34 = (f32[1024]{0:T(1024)S(1)}, f32[1024]{0:T(1024)}, u32[]{:S(2)}) copy-start(f32[1024]{0:T(1024)} %param.32) | copy-start | bytes 12292
  64.4 33.2 %all-gather.11.cloned.1.call-start = ((), (), s32[]{:S(2)}) async-start(), calls=%async_computation.13 | async-start | bytes 2359296 | tf_op jit(solution)/shard_map/all_gather | solution.py:232
  65.0 59.7 %all-gather.9.cloned.1.call-start = ((), (), s32[]{:S(2)}) async-start(), calls=%async_computation.12 | async-start | bytes 1310720 | tf_op jit(solution)/shard_map/all_gather | solution.py:230
  96.3 57.5 %all-gather.13.cloned.1.call-start = ((), (), s32[]{:S(2)}) async-start(), calls=%async_computation.14 | async-start | bytes 2359296 | tf_op jit(solution)/shard_map/all_gather | solution.py:233
  96.9 88.2 %reduce-scatter.13.cloned.1.call-start = ((), (), s32[]{:S(2)}) async-start(), calls=%async_computation.15 | async-start | bytes 1310720 | tf_op jit(solution)/shard_map/reduce_scatter | solution.py:239
  129.3 28.3 %copy-start.25 = (bf16[512,1024]{1,0:T(8,128)(2,1)}, bf16[512,1024]{1,0:T(8,128)(2,1)S(1)}, u32[]{:S(2)}) copy-start(bf16[512,1024]{1,0:T(8,128)(2,1)S(1)} %get-tuple-element.629) | copy-start | bytes 3145732
  153.8 31.3 %copy-start.11 = (bf16[128,1024]{1,0:T(8,128)(2,1)S(1)}, bf16[128,1024]{1,0:T(8,128)(2,1)}, u32[]{:S(2)}) copy-start(bf16[128,1024]{1,0:T(8,128)(2,1)} %reduce-scatter.11.cloned.1.call-done) | copy-start | bytes 786436
  153.8 31.3 %copy-start.40 = (f32[1024]{0:T(1024)S(1)}, f32[1024]{0:T(1024)}, u32[]{:S(2)}) copy-start(f32[1024]{0:T(1024)} %param.36) | copy-start | bytes 12292
  157.6 29.0 %copy-start.28 = (bf16[128,1024]{1,0:T(8,128)(2,1)S(1)}, bf16[128,1024]{1,0:T(8,128)(2,1)}, u32[]{:S(2)}) copy-start(bf16[128,1024]{1,0:T(8,128)(2,1)} %param.39) | copy-start | bytes 786436
  157.6 29.0 %copy-start.35 = (f32[1024]{0:T(1024)S(1)}, f32[1024]{0:T(1024)}, u32[]{:S(2)}) copy-start(f32[1024]{0:T(1024)} %param.37) | copy-start | bytes 12292
  157.6 29.4 %copy-start.41 = (f32[1024]{0:T(1024)S(1)}, f32[1024]{0:T(1024)}, u32[]{:S(2)}) copy-start(f32[1024]{0:T(1024)} %param.38) | copy-start | bytes 12292
  157.7 57.1 %all-gather.15.cloned.1.call-start = ((), (), s32[]{:S(2)}) async-start(), calls=%async_computation.16 | async-start | bytes 1310720 | tf_op jit(solution)/shard_map/all_gather | solution.py:261
  188.1 61.9 %reduce-scatter.15.cloned.1.call-start = ((), (), s32[]{:S(2)}) async-start(), calls=%async_computation.17 | async-start | bytes 1310720 | tf_op jit(solution)/shard_map/reduce_scatter | solution.py:267
  214.7 6.1 %copy-start.43 = (bf16[1024,1024]{1,0:T(8,128)(2,1)S(1)}, bf16[1024,1024]{1,0:T(8,128)(2,1)}, u32[]{:S(2)}) copy-start(bf16[1024,1024]{1,0:T(8,128)(2,1)} %all-gather.11.cloned.1.call-done) | copy-start | bytes 6291460
  223.2 58.0 %all-gather.17.cloned.1.call-start = ((), (), s32[]{:S(2)}) async-start(), calls=%async_computation.18 | async-start | bytes 1310720 | tf_op jit(solution)/shard_map/all_gather | solution.py:281
  250.0 31.2 %copy-start.18 = (bf16[256,1024]{1,0:T(8,128)(2,1)S(1)}, bf16[256,1024]{1,0:T(8,128)(2,1)}, u32[]{:S(2)}) copy-start(bf16[256,1024]{1,0:T(8,128)(2,1)} %all_gather.40) | copy-start | bytes 1572868
  253.8 29.8 %copy-start.14 = (f32[128,1024]{1,0:T(8,128)}, f32[128,1024]{1,0:T(8,128)S(1)}, u32[]{:S(2)}) copy-start(f32[128,1024]{1,0:T(8,128)S(1)} %get-tuple-element.615) | copy-start | bytes 1572868
  254.7 108.1 %reduce-scatter.19.cloned.1.call-start = ((), (), s32[]{:S(2)}) async-start(), calls=%async_computation.20 | async-start | bytes 1179648 | tf_op jit(solution)/shard_map/reduce_scatter | solution.py:305
  284.7 1.9 copy-start
  284.7 1.9 copy-start.23
  286.8 2.4 copy-start.1
  291.3 1.9 copy-start
  291.3 1.9 copy-start.23
  293.3 2.4 copy-start.1
  297.7 3.0 copy-start.10
  300.6 74.5 %reduce-scatter.21.cloned.1.call-start = ((), (), s32[]{:S(2)}) async-start(), calls=%async_computation.21 | async-start | bytes 1179648 | tf_op jit(solution)/shard_map/reduce_scatter | solution.py:306
  302.2 1.6 copy-start.22
  302.2 111.9 %reduce-scatter.23.cloned.1.call-start = ((), (), s32[]{:S(2)}) async-start(), calls=%async_computation.22 | async-start | bytes 1179648 | tf_op jit(solution)/shard_map/reduce_scatter | solution.py:307
  303.7 139.8 %reduce-scatter.17.cloned.1.call-start = ((), (), s32[]{:S(2)}) async-start(), calls=%async_computation.19 | async-start | bytes 1310720 | tf_op jit(solution)/shard_map/reduce_scatter | solution.py:298
  304.8 1.6 copy-start.17
  307.9 173.7 %reduce-scatter.25.cloned.1.call-start = ((), (), s32[]{:S(2)}) async-start(), calls=%async_computation.23 | async-start | bytes 1179648 | tf_op jit(solution)/shard_map/reduce_scatter | solution.py:308
  309.4 227.1 %reduce-scatter.29.cloned.1.call-start = ((), (), s32[]{:S(2)}) async-start(), calls=%async_computation.25 | async-start | bytes 4718592 | tf_op jit(solution)/shard_map/reduce_scatter | solution.py:275
  314.0 277.3 %reduce-scatter.27.cloned.1.call-start = ((), (), s32[]{:S(2)}) async-start(), calls=%async_computation.24 | async-start | bytes 4718592 | tf_op jit(solution)/shard_map/reduce_scatter | solution.py:274
  318.8 2.6 copy-start.36
  318.8 2.6 copy-start.37
  318.8 2.6 copy-start.38
  318.8 2.6 copy-start.39
  318.8 124.8 %copy-start.15 = (f32[128,1024]{1,0:T(8,128)S(1)}, f32[128,1024]{1,0:T(8,128)}, u32[]{:S(2)}) copy-start(f32[128,1024]{1,0:T(8,128)} %copy-done.14) | copy-start | bytes 1572868
  (23 other events, 27.1 us)
Sparse Core Ops, SparseCore 0:
  10.4 30.6 all-gather.6
  64.5 27.5 reduce-scatter.10
  157.8 27.2 reduce-scatter.12
  188.2 26.4 all-gather.14
  223.3 26.6 reduce-scatter.14
Sparse Core Ops, SparseCore 1:
  66.8 27.9 all-gather.10
  96.8 27.9 all-gather.8
  126.4 27.3 all-gather.12
  254.7 26.4 all-gather.16
  300.7 35.2 reduce-scatter.18
  339.2 35.9 reduce-scatter.20
  378.2 35.9 reduce-scatter.22
  416.3 27.2 reduce-scatter.16
  447.2 34.3 reduce-scatter.24
  485.5 50.9 reduce-scatter.28
  540.3 50.9 reduce-scatter.26
where the time goes:
time: 600 us; the launch traced here: 599 us
  waiting for transfers between devices  409 us (68%)
  blocking collectives  82.3 us (14%)
  matrix products  48.7 us (8%)
  other arithmetic  21.4 us (4%)
  local copies, waits for them, and re-layouts  17.9 us (3%)
  between operations  17.3 us (3%)
    reduce_scatter x1, waiting for transfers between devices, on_device(): lax.psum_scatter(grad_w_back, 'dp', scatter_dimension=1, tiled=True)  54.9 us
    reduce_scatter x1, waiting for transfers between devices, on_device(): lax.psum_scatter(grad_w_in, 'dp', scatter_dimension=0, tiled=True)  54.8 us
    psum x1, blocking collectives, on_device(): lax.psum((widen(grad_b_query_part, b_query.shape[0]), widen(grad_b_value_...  41.4 us
    reduce_scatter x1, waiting for transfers between devices, on_device(): lax.psum_scatter(grad_w_value, 'dp', scatter_dimension=0, tiled=True)  37.3 us
    reduce_scatter x1, waiting for transfers between devices, on_device(): lax.psum_scatter(grad_w_out, 'dp', scatter_dimension=1, tiled=True)  36.2 us
    reduce_scatter x1, waiting for transfers between devices, on_device(): lax.psum_scatter((query_part + key_part + value_part).astype(jnp.bfloat16...  27.8 us
    reduce_scatter x1, waiting for transfers between devices, on_device(): lax.psum_scatter(matmul_plain(activation, mat_back).astype(jnp.bfloat16),...  27.4 us
    reduce_scatter x1, waiting for transfers between devices, on_device(): lax.psum_scatter(matmul_plain(context, mat_out).astype(jnp.bfloat16), 'te...  27.1 us
  transfers between devices with their start and end apart: 16, of which 13 were waited for; matrix products, arithmetic and copies ran while one was open for 6% of the time, Pallas kernels for 0%

commit v1 on v0

--- a/solution.py
+++ b/solution.py
@@ -6,6 +6,28 @@
 HD = 64
 epsilon = 1e-06
 masked_value = -1e30
+
+
+def in_order(pieces, dim):
+    shape = list(pieces.shape[1:])
+    shape[dim] *= pieces.shape[0]
+    return jnp.moveaxis(pieces, 0, dim).reshape(shape)
+
+
+def grow_blocks(x, axis):
+    size = lax.axis_size(axis)
+    blocks = x[None]
+    for level in range(size.bit_length() - 1):
+        bit = 1 << level
+        other = lax.ppermute(blocks, axis, [(i, i ^ bit) for i in range(size)])
+        both = jnp.stack([blocks, other])
+        upper = lax.axis_index(axis) >> level & 1
+        blocks = jnp.where(upper == 0, both, both[::-1]).reshape(-1, *x.shape)
+    return blocks
+
+
+def gather_by_bits(array, axis, dim):
+    return in_order(grow_blocks(array, axis), dim)
 
 
 def matmul_plain(left_side, right_side):
@@ -278,7 +300,7 @@
     grad_shift_attn = jnp.sum(grad_one_out, axis=0)
     grad_one = norm_back(grad_one_out, normed_one, inv_one, gain_attn)
     grad_b_out = jnp.sum(grad_one, axis=0)
-    grad_one_full = lax.all_gather(grad_one.astype(jnp.bfloat16), "tensor", axis=0, tiled=True)
+    grad_one_full = gather_by_bits(grad_one.astype(jnp.bfloat16), "tensor", 0)
     grad_w_out = matmul_over_rows(context, grad_one_full)
     grad_context = matmul_over_cols(grad_one_full, mat_out).astype(jnp.bfloat16)
     grad_query, grad_keys, grad_values = attend_backward(

time: 600 us -> 604 us (level)
  waiting for transfers between devices: 409 us -> 416 us
    ppermute x0 -> x2, waiting for transfers between devices: none -> 30.9 us  [grow_blocks(): other = lax.ppermute(blocks, axis, [(i, i ^ bit) for i in range(size)])]
    all_gather x1 -> x0, waiting for transfers between devices: 26.5 us -> none  [on_device(): lax.all_gather(grad_one.astype(jnp.bfloat16), 'tensor', axis=0, tiled=True)]
  transfers between devices with their start and end apart: 16 -> 17, of which waited for: 13 -> 14; matrix products, arithmetic and copies ran while one was open for 6% -> 6% of each run, Pallas kernels for 0% -> 0%
where the time goes in v1:
time: 604 us; the launch traced here: 603 us
  waiting for transfers between devices  416 us (69%)
  blocking collectives  80.1 us (13%)
  matrix products  47.5 us (8%)
  other arithmetic  21.1 us (3%)
  local copies, waits for them, and re-layouts  18.6 us (3%)
  between operations  17.1 us (3%)
    reduce_scatter x1, waiting for transfers between devices, on_device(): lax.psum_scatter(grad_w_in, 'dp', scatter_dimension=0, tiled=True)  55 us
    reduce_scatter x1, waiting for transfers between devices, on_device(): lax.psum_scatter(grad_w_back, 'dp', scatter_dimension=1, tiled=True)  54.7 us
    psum x1, blocking collectives, on_device(): lax.psum((widen(grad_b_query_part, b_query.shape[0]), widen(grad_b_value_...  39.2 us
    reduce_scatter x1, waiting for transfers between devices, on_device(): lax.psum_scatter(grad_w_value, 'dp', scatter_dimension=0, tiled=True)  37.5 us
    reduce_scatter x1, waiting for transfers between devices, on_device(): lax.psum_scatter(grad_w_out, 'dp', scatter_dimension=1, tiled=True)  36.2 us
    ppermute x2, waiting for transfers between devices, grow_blocks(): other = lax.ppermute(blocks, axis, [(i, i ^ bit) for i in range(size)])  30.9 us
    reduce_scatter x1, waiting for transfers between devices, on_device(): lax.psum_scatter((query_part + key_part + value_part).astype(jnp.bfloat16...  27.7 us
    reduce_scatter x1, waiting for transfers between devices, on_device(): lax.psum_scatter(matmul_plain(activation, mat_back).astype(jnp.bfloat16),...  27.4 us
  transfers between devices with their start and end apart: 17, of which 14 were waited for; matrix products, arithmetic and copies ran while one was open for 6% of the time, Pallas kernels for 0%

profile of v1, /device:TPU:0, one launch (start us, length us, event | category | flops | bytes accessed | tf_op | source)
XLA Modules:
  0.0 603.0 jit_solution(1646159791712587952)
XLA Ops:
  10.3 1.3 fusion.38
  13.0 11.6 %all_gather.34 = bf16[1024,256]{1,0:T(8,128)(2,1)S(1)} all-gather(bf16[128,256]{1,0:T(8,128)(2,1)} %param.27), channel_id=1, replica_groups=mesh['dp'=8,'tensor'=4] {'dp'}, dimensions={0}, use_global_device_ids=true | all-gather | bytes 589824 | tf_op jit(solution)/shard_map/all_gather | solution.py:232
  24.6 9.5 %all_gather.35 = bf16[1024,256]{1,0:T(8,128)(2,1)S(1)} all-gather(bf16[128,256]{1,0:T(8,128)(2,1)} %param.24), channel_id=1, replica_groups=mesh['dp'=8,'tensor'=4] {'dp'}, dimensions={0}, use_global_device_ids=true | all-gather | bytes 589824 | tf_op jit(solution)/shard_map/all_gather | solution.py:230
  34.1 9.2 %all_gather.36 = bf16[1024,256]{1,0:T(8,128)(2,1)S(1)} all-gather(bf16[128,256]{1,0:T(8,128)(2,1)} %param.26), channel_id=1, replica_groups=mesh['dp'=8,'tensor'=4] {'dp'}, dimensions={0}, use_global_device_ids=true | all-gather | bytes 589824 | tf_op jit(solution)/shard_map/all_gather | solution.py:231
  43.3 10.6 %all_gather.37 = bf16[256,1024]{1,0:T(8,128)(2,1)} all-gather(bf16[256,128]{1,0:T(8,128)(2,1)S(1)} %copy-done.34), channel_id=1, replica_groups=mesh['dp'=8,'tensor'=4] {'dp'}, dimensions={1}, use_global_device_ids=true | all-gather | bytes 589824 | tf_op jit(solution)/shard_map/all_gather | solution.py:233
  53.9 1.8 fusion.13
  57.1 4.8 while.38
  61.9 2.5 convolution_convert_fusion.3
  65.0 27.1 %reduce-scatter.11.cloned.1.call-done = bf16[128,1024]{1,0:T(8,128)(2,1)} async-done(((bf16[512,1024]{1,0:T(8,128)(2,1)}), bf16[128,1024]{1,0:T(8,128)(2,1)}) %reduce-scatter.11.cloned.1.call-update) | async-done | bytes 262160 | tf_op jit(solution)/shard_map/reduce_scatter | solution.py:243
  93.3 1.2 multiply_reduce_fusion.5
  94.4 1.8 fusion.21
  97.6 27.1 %all-gather.8.cloned.1.call-done = bf16[512,1024]{1,0:T(8,128)(2,1)} async-done(((bf16[128,1024]{1,0:T(8,128)(2,1)}), bf16[512,1024]{1,0:T(8,128)(2,1)}) %all-gather.8.cloned.1.call-update) | async-done | bytes 1048592 | tf_op jit(solution)/shard_map/all_gather | solution.py:252
  124.7 4.6 multiply_convert_fusion.1
  129.3 24.4 %all-gather.12.cloned.1.call-done = bf16[1024,1024]{1,0:T(8,128)(2,1)} async-done(((bf16[1024,128]{1,0:T(8,128)(2,1)}), bf16[1024,1024]{1,0:T(8,128)(2,1)}) %all-gather.12.cloned.1.call-update) | async-done | bytes 2097168 | tf_op jit(solution)/shard_map/all_gather | solution.py:255
  153.8 3.9 convolution_convert_fusion.2
  157.7 27.4 %reduce-scatter.13.cloned.1.call-done = bf16[128,1024]{1,0:T(8,128)(2,1)} async-done(((bf16[512,1024]{1,0:T(8,128)(2,1)}), bf16[128,1024]{1,0:T(8,128)(2,1)}) %reduce-scatter.13.cloned.1.call-update) | async-done | bytes 262160 | tf_op jit(solution)/shard_map/reduce_scatter | solution.py:261
  185.1 1.3 fusion.36
  188.3 26.4 %all-gather.14.cloned.1.call-done = bf16[512,1024]{1,0:T(8,128)(2,1)} async-done(((bf16[128,1024]{1,0:T(8,128)(2,1)}), bf16[512,1024]{1,0:T(8,128)(2,1)}) %all-gather.14.cloned.1.call-update) | async-done | bytes 1048592 | tf_op jit(solution)/shard_map/all_gather | solution.py:283
  214.7 5.2 fusion.39
  220.9 2.3 convolution_convert_fusion.1
  223.3 26.8 %reduce-scatter.15.cloned.1.call-done = bf16[128,1024]{1,0:T(8,128)(2,1)} async-done(((bf16[512,1024]{1,0:T(8,128)(2,1)}), bf16[128,1024]{1,0:T(8,128)(2,1)}) %reduce-scatter.15.cloned.1.call-update) | async-done | bytes 262160 | tf_op jit(solution)/shard_map/reduce_scatter | solution.py:289
  250.1 1.9 multiply_reduce_fusion.1
  252.0 1.8 fusion.34
  253.9 7.6 %collective-permute-done = bf16[1,128,1024]{2,1,0:T(8,128)(2,1)S(1)} collective-permute-done((bf16[1,128,1024]{2,1,0:T(8,128)(2,1)S(1)}, bf16[1,128,1024]{2,1,0:T(8,128)(2,1)S(1)}, u32[]{:S(2)}, u32[]{:S(2)}) %collective-permute-start) | collective-permute-done | bytes 262176 | tf_op jit(solution)/shard_map/ppermute | solution.py:22
  261.8 1.3 collective-permute-start.1
  263.1 23.3 %collective-permute-done.1 = bf16[2,128,1024]{2,1,0:T(8,128)(2,1)S(1)} collective-permute-done((bf16[2,128,1024]{2,1,0:T(8,128)(2,1)S(1)}, bf16[2,128,1024]{2,1,0:T(8,128)(2,1)S(1)}, u32[]{:S(2)}, u32[]{:S(2)}) %collective-permute-start.1) | collective-permute-done | bytes 524320 | tf_op jit(solution)/shard_map/ppermute | solution.py:22
  287.5 1.2 convolution_convert_fusion.4
  289.7 13.1 %while.39 = (s32[]{:T(128)}, f32[512,256]{0,1:T(8,128)}, f32[512,256]{0,1:T(8,128)S(1)}, f32[512,256]{0,1:T(8,128)S(1)}, bf16[512,256]{0,1:T(8,128)(2,1)S(1)}, /...) while((s32[]{:T(128)}, f32[512,256]{0,1:T(8,128)}, ...), condition=%wide.region_17.18_spmd.clone, body=%wide.region_15.17_spmd.clone.sunk | while | flops 340395520 | bytes 25846364 | solution.py:190
  302.8 2.9 convolution_bitcast_fusion.2
  305.7 1.5 convolution_bitcast_fusion.1
  307.3 1.5 convolution_bitcast_fusion
  309.8 1.6 fusion.31
  311.4 1.5 add_convert_fusion
  313.0 1.4 fusion.42
  314.5 4.5 fusion.43
  320.5 3.3 fusion.15
  324.7 1.2 reduce_sum.193
  326.4 39.2 %all-reduce = (f32[1024]{0:T(1024)}, f32[1024]{0:T(1024)}, f32[1024]{0:T(1024)}, f32[1024]{0:T(1024)}, f32[1024]{0:T(1024)}, /*index=5*/f32[4096]{0:T(1024)}, f32[1024]{0:T(1024)}, f32[1024]{0:T(1024)}, f32[1024]{0:T(1024)}) all-reduce(f32[1024]{0:T(1024)S(1)} %dynamic_update_slice.62, ...), channel_id=1, replica_groups=mesh['dp'=8,'tensor'=4] {'dp','tensor'}, use_global_device_ids=true, to_apply=%region_21.22 | all-reduce | flops 12288 | bytes 98304 | tf_op jit(solution)/shard_map/psum | solution.py:338
  365.6 1.7 copy.43
  367.3 12.4 %reduce-scatter.21.cloned.1.call-done = f32[128,256]{0,1:T(8,128)} async-done(((f32[1024,256]{0,1:T(8,128)}), f32[128,256]{0,1:T(8,128)}) %reduce-scatter.21.cloned.1.call-update) | async-done | bytes 131088 | tf_op jit(solution)/shard_map/reduce_scatter | solution.py:328
  379.6 1.7 copy.44
  381.3 37.5 %reduce-scatter.23.cloned.1.call-done = f32[128,256]{0,1:T(8,128)} async-done(((f32[1024,256]{0,1:T(8,128)}), f32[128,256]{0,1:T(8,128)}) %reduce-scatter.23.cloned.1.call-update) | async-done | bytes 131088 | tf_op jit(solution)/shard_map/reduce_scatter | solution.py:329
  418.8 1.7 copy.45
  420.4 27.7 %reduce-scatter.17.cloned.1.call-done = bf16[128,1024]{1,0:T(8,128)(2,1)} async-done(((bf16[512,1024]{1,0:T(8,128)(2,1)}), bf16[128,1024]{1,0:T(8,128)(2,1)}) %reduce-scatter.17.cloned.1.call-update) | async-done | bytes 262160 | tf_op jit(solution)/shard_map/reduce_scatter | solution.py:320
  448.2 1.8 convert_add_fusion.2
  450.0 36.2 %reduce-scatter.25.cloned.1.call-done = f32[256,128]{1,0:T(8,128)} async-done(((f32[256,1024]{1,0:T(8,128)}), f32[256,128]{1,0:T(8,128)}) %reduce-scatter.25.cloned.1.call-update) | async-done | bytes 131088 | tf_op jit(solution)/shard_map/reduce_scatter | solution.py:330
  486.2 54.7 %reduce-scatter.29.cloned.1.call-done = f32[1024,128]{1,0:T(8,128)} async-done(((f32[1024,1024]{1,0:T(8,128)}), f32[1024,128]{1,0:T(8,128)}) %reduce-scatter.29.cloned.1.call-update) | async-done | bytes 524304 | tf_op jit(solution)/shard_map/reduce_scatter | solution.py:297
  540.9 55.0 %reduce-scatter.27.cloned.1.call-done = f32[128,1024]{1,0:T(8,128)} async-done(((f32[1024,1024]{1,0:T(8,128)}), f32[128,1024]{1,0:T(8,128)}) %reduce-scatter.27.cloned.1.call-update) | async-done | bytes 524304 | tf_op jit(solution)/shard_map/reduce_scatter | solution.py:296
  (234 shorter events, 33.5 us)
Async XLA Ops:
  8.0 35.3 %copy-start.34 = (bf16[256,128]{1,0:T(8,128)(2,1)S(1)}, bf16[256,128]{1,0:T(8,128)(2,1)}, u32[]{:S(2)}) copy-start(bf16[256,128]{1,0:T(8,128)(2,1)} %param.29) | copy-start | bytes 196612
  8.0 45.8 %all-gather.6.cloned.1.call-start = ((), (), s32[]{:S(2)}) async-start(), calls=%async_computation.10 | async-start | bytes 1310720 | tf_op jit(solution)/shard_map/all_gather | solution.py:228
  8.8 83.4 %reduce-scatter.11.cloned.1.call-start = ((), (), s32[]{:S(2)}) async-start(), calls=%async_computation.11 | async-start | bytes 1310720 | tf_op jit(solution)/shard_map/reduce_scatter | solution.py:243
  24.6 31.2 %copy-start.18 = (bf16[1024,256]{1,0:T(8,128)(2,1)}, bf16[1024,256]{1,0:T(8,128)(2,1)S(1)}, u32[]{:S(2)}) copy-start(bf16[1024,256]{1,0:T(8,128)(2,1)S(1)} %all_gather.34) | copy-start | bytes 1572868
  34.1 22.2 %copy-start.21 = (bf16[1024,256]{1,0:T(8,128)(2,1)}, bf16[1024,256]{1,0:T(8,128)(2,1)S(1)}, u32[]{:S(2)}) copy-start(bf16[1024,256]{1,0:T(8,128)(2,1)S(1)} %all_gather.35) | copy-start | bytes 1572868
  43.3 13.1 %copy-start.23 = (bf16[1024,256]{1,0:T(8,128)(2,1)}, bf16[1024,256]{1,0:T(8,128)(2,1)S(1)}, u32[]{:S(2)}) copy-start(bf16[1024,256]{1,0:T(8,128)(2,1)S(1)} %all_gather.36) | copy-start | bytes 1572868
  53.9 1.9 copy-start.9
  61.8 30.3 %copy-start.2 = (bf16[128,1024]{1,0:T(8,128)(2,1)S(1)}, bf16[128,1024]{1,0:T(8,128)(2,1)}, u32[]{:S(2)}) copy-start(bf16[128,1024]{1,0:T(8,128)(2,1)} %param.22) | copy-start | bytes 786436
  61.9 30.3 %copy-start.32 = (f32[1024]{0:T(1024)S(1)}, f32[1024]{0:T(1024)}, u32[]{:S(2)}) copy-start(f32[1024]{0:T(1024)} %param.30) | copy-start | bytes 12292
  61.9 32.6 %copy-start.33 = (f32[1024]{0:T(1024)S(1)}, f32[1024]{0:T(1024)}, u32[]{:S(2)}) copy-start(f32[1024]{0:T(1024)} %param.31) | copy-start | bytes 12292
  61.9 32.6 %copy-start.35 = (f32[1024]{0:T(1024)S(1)}, f32[1024]{0:T(1024)}, u32[]{:S(2)}) copy-start(f32[1024]{0:T(1024)} %param.32) | copy-start | bytes 12292
  64.4 33.2 %all-gather.10.cloned.1.call-start = ((), (), s32[]{:S(2)}) async-start(), calls=%async_computation.13 | async-start | bytes 2359296 | tf_op jit(solution)/shard_map/all_gather | solution.py:254
  65.0 59.7 %all-gather.8.cloned.1.call-start = ((), (), s32[]{:S(2)}) async-start(), calls=%async_computation.12 | async-start | bytes 1310720 | tf_op jit(solution)/shard_map/all_gather | solution.py:252
  96.3 57.5 %all-gather.12.cloned.1.call-start = ((), (), s32[]{:S(2)}) async-start(), calls=%async_computation.14 | async-start | bytes 2359296 | tf_op jit(solution)/shard_map/all_gather | solution.py:255
  96.9 88.2 %reduce-scatter.13.cloned.1.call-start = ((), (), s32[]{:S(2)}) async-start(), calls=%async_computation.15 | async-start | bytes 1310720 | tf_op jit(solution)/shard_map/reduce_scatter | solution.py:261
  129.3 28.3 %copy-start.27 = (bf16[512,1024]{1,0:T(8,128)(2,1)}, bf16[512,1024]{1,0:T(8,128)(2,1)S(1)}, u32[]{:S(2)}) copy-start(bf16[512,1024]{1,0:T(8,128)(2,1)S(1)} %get-tuple-element.633) | copy-start | bytes 3145732
  153.7 31.4 %copy-start.11 = (bf16[128,1024]{1,0:T(8,128)(2,1)S(1)}, bf16[128,1024]{1,0:T(8,128)(2,1)}, u32[]{:S(2)}) copy-start(bf16[128,1024]{1,0:T(8,128)(2,1)} %reduce-scatter.11.cloned.1.call-done) | copy-start | bytes 786436
  153.8 31.4 %copy-start.41 = (f32[1024]{0:T(1024)S(1)}, f32[1024]{0:T(1024)}, u32[]{:S(2)}) copy-start(f32[1024]{0:T(1024)} %param.36) | copy-start | bytes 12292
  157.6 29.0 %copy-start.29 = (bf16[128,1024]{1,0:T(8,128)(2,1)S(1)}, bf16[128,1024]{1,0:T(8,128)(2,1)}, u32[]{:S(2)}) copy-start(bf16[128,1024]{1,0:T(8,128)(2,1)} %param.39) | copy-start | bytes 786436
  157.6 29.0 %copy-start.36 = (f32[1024]{0:T(1024)S(1)}, f32[1024]{0:T(1024)}, u32[]{:S(2)}) copy-start(f32[1024]{0:T(1024)} %param.37) | copy-start | bytes 12292
  157.6 29.4 %copy-start.42 = (f32[1024]{0:T(1024)S(1)}, f32[1024]{0:T(1024)}, u32[]{:S(2)}) copy-start(f32[1024]{0:T(1024)} %param.38) | copy-start | bytes 12292
  157.7 57.1 %all-gather.14.cloned.1.call-start = ((), (), s32[]{:S(2)}) async-start(), calls=%async_computation.16 | async-start | bytes 1310720 | tf_op jit(solution)/shard_map/all_gather | solution.py:283
  188.1 62.0 %reduce-scatter.15.cloned.1.call-start = ((), (), s32[]{:S(2)}) async-start(), calls=%async_computation.17 | async-start | bytes 1310720 | tf_op jit(solution)/shard_map/reduce_scatter | solution.py:289
  214.7 6.2 %copy-start.44 = (bf16[1024,1024]{1,0:T(8,128)(2,1)S(1)}, bf16[1024,1024]{1,0:T(8,128)(2,1)}, u32[]{:S(2)}) copy-start(bf16[1024,1024]{1,0:T(8,128)(2,1)} %all-gather.10.cloned.1.call-done) | copy-start | bytes 6291460
  223.2 142.4 %reduce-scatter.19.cloned.1.call-start = ((), (), s32[]{:S(2)}) async-start(), calls=%async_computation.19 | async-start | bytes 1179648 | tf_op jit(solution)/shard_map/reduce_scatter | solution.py:327
  253.8 32.7 %copy-start.14 = (f32[128,1024]{1,0:T(8,128)}, f32[128,1024]{1,0:T(8,128)S(1)}, u32[]{:S(2)}) copy-start(f32[128,1024]{1,0:T(8,128)S(1)} %get-tuple-element.615) | copy-start | bytes 1572868
  253.9 7.7 %collective-permute-start = (bf16[1,128,1024]{2,1,0:T(8,128)(2,1)S(1)}, bf16[1,128,1024]{2,1,0:T(8,128)(2,1)S(1)}, u32[]{:S(2)}, u32[]{:S(2)}) collective-permute-start(bf16[1,128,1024]{2,1,0:T(8,128)(2,1)S(1)} %get-tuple-element.630), channel_id=1, source_target_pairs={{0,1},{1,0},{2,3},{3,2},{4,5},{5,4},{6,7},{7,6},{8,9},{9,8},{10,11... | collective-permute-start | bytes 786440 | tf_op jit(solution)/shard_map/ppermute | solution.py:22
  261.8 24.6 %collective-permute-start.1 = (bf16[2,128,1024]{2,1,0:T(8,128)(2,1)S(1)}, bf16[2,128,1024]{2,1,0:T(8,128)(2,1)S(1)}, u32[]{:S(2)}, u32[]{:S(2)}) collective-permute-start(bf16[2,128,1024]{2,1,0:T(8,128)(2,1)S(1)} %get-tuple-element.628), channel_id=1, source_target_pairs={{0,2},{1,3},{2,0},{3,1},{4,6},{5,7},{6,4},{7,5},{8,10},{9,11},{10,... | collective-permute-start | bytes 1572872 | tf_op jit(solution)/shard_map/ppermute | solution.py:22
  286.8 2.9 copy-start.16
  289.8 1.9 copy-start
  289.8 1.9 copy-start.25
  291.8 2.4 copy-start.1
  296.3 1.9 copy-start
  296.3 1.9 copy-start.25
  298.4 2.4 copy-start.1
  302.8 3.0 copy-start.10
  305.7 74.0 %reduce-scatter.21.cloned.1.call-start = ((), (), s32[]{:S(2)}) async-start(), calls=%async_computation.20 | async-start | bytes 1179648 | tf_op jit(solution)/shard_map/reduce_scatter | solution.py:328
  307.2 1.6 copy-start.24
  307.2 111.6 %reduce-scatter.23.cloned.1.call-start = ((), (), s32[]{:S(2)}) async-start(), calls=%async_computation.21 | async-start | bytes 1179648 | tf_op jit(solution)/shard_map/reduce_scatter | solution.py:329
  308.8 139.4 %reduce-scatter.17.cloned.1.call-start = ((), (), s32[]{:S(2)}) async-start(), calls=%async_computation.18 | async-start | bytes 1310720 | tf_op jit(solution)/shard_map/reduce_scatter | solution.py:320
  312.9 173.3 %reduce-scatter.25.cloned.1.call-start = ((), (), s32[]{:S(2)}) async-start(), calls=%async_computation.22 | async-start | bytes 1179648 | tf_op jit(solution)/shard_map/reduce_scatter | solution.py:330
  314.4 226.5 %reduce-scatter.29.cloned.1.call-start = ((), (), s32[]{:S(2)}) async-start(), calls=%async_computation.24 | async-start | bytes 4718592 | tf_op jit(solution)/shard_map/reduce_scatter | solution.py:297
  319.0 276.9 %reduce-scatter.27.cloned.1.call-start = ((), (), s32[]{:S(2)}) async-start(), calls=%async_computation.23 | async-start | bytes 4718592 | tf_op jit(solution)/shard_map/reduce_scatter | solution.py:296
  323.8 2.6 copy-start.37
  323.8 2.6 copy-start.38
  323.8 2.6 copy-start.39
  323.8 2.6 copy-start.40
  323.8 124.4 %copy-start.15 = (f32[128,1024]{1,0:T(8,128)S(1)}, f32[128,1024]{1,0:T(8,128)}, u32[]{:S(2)}) copy-start(f32[128,1024]{1,0:T(8,128)} %copy-done.14) | copy-start | bytes 1572868
  (25 other events, 29.7 us)
Sparse Core Ops, SparseCore 0:
  10.4 30.6 all-gather.5
  64.5 27.5 reduce-scatter.10
  157.8 27.2 reduce-scatter.12
  188.2 26.4 all-gather.13
  223.3 26.6 reduce-scatter.14
Sparse Core Ops, SparseCore 1:
  66.8 27.9 all-gather.9
  96.7 27.9 all-gather.7
  126.4 27.3 all-gather.11
  305.8 34.7 reduce-scatter.18
  343.8 35.8 reduce-scatter.20
  382.8 35.9 reduce-scatter.22
  420.9 27.2 reduce-scatter.16
  451.8 34.3 reduce-scatter.24
  490.0 50.9 reduce-scatter.28
  544.9 51.0 reduce-scatter.26
